TPU v7x, 32 devices: a whole 2x2x4 slice. The times are simulated.
32 devices in a mesh: owner: 16 (over z, y, core), rows: 2 (over x).
Axes of the slice: x: 2, y: 2, z: 4, core: 2. Of those that a mesh axis runs over, the one named last changes fastest.
Arguments:
- w_gate: float32 [64, 2048, 1024], P('owner', 'rows'), may hold values from -0.1875 to 0.1875
- avg_gate: float32 [64, 2048, 1024], P('owner', 'rows'), may hold values from -0.125 to 0.125
- w_up: float32 [64, 2048, 1024], P('owner', 'rows'), may hold values from -0.1875 to 0.1875
- avg_up: float32 [64, 2048, 1024], P('owner', 'rows'), may hold values from -0.125 to 0.125
- mix_share: float32 [64], P('owner'), may hold values from 0.2 to 0.8
- router_weight: float32 [2048, 64], P('rows', 'owner'), may hold values from -0.125 to 0.125
- router_gain: float32 [2048], P('rows'), may hold values from 0.25 to 1.75
Outputs:
- serve_gate: bfloat16 [64, 2048, 1024], P('owner')
- serve_up: bfloat16 [64, 2048, 1024], P('owner')
- scale_gate: float32 [64, 1024], P('owner')
- scale_up: float32 [64, 1024], P('owner')
- serve_router: bfloat16 [2048, 64], replicated
All inputs are finite; a program needn't handle non-finite values.
Results may differ from a plain program's by a relative error of at most 0.0015.
Values may be sent and summed in bfloat16 or wider, within the bound.
A program may use at most 192 MiB of HBM per device.

v0:
```python
import jax
import jax.numpy as jnp
from jax import lax
from jax.sharding import PartitionSpec as P


def shards(w_gate, avg_gate, w_up, avg_up, mix_share, router_weight, router_gain):
    fresh_gate = mix_share[:, None, None] * w_gate + (1.0 - mix_share[:, None, None]) * avg_gate
    fresh_up = mix_share[:, None, None] * w_up + (1.0 - mix_share[:, None, None]) * avg_up
    total_gate, total_up = lax.psum(
        (jnp.sum(fresh_gate * fresh_gate, axis=1), jnp.sum(fresh_up * fresh_up, axis=1)), "rows"
    )
    scale_gate = jnp.sqrt(total_gate)
    scale_up = jnp.sqrt(total_up)
    narrow_gate, narrow_up = (
        (fresh_gate / jnp.expand_dims(scale_gate, 1)).astype(jnp.bfloat16),
        (fresh_up / jnp.expand_dims(scale_up, 1)).astype(jnp.bfloat16),
    )
    serve_gate, serve_up = (
        lax.all_gather(narrow_gate, "rows", axis=1, tiled=True),
        lax.all_gather(narrow_up, "rows", axis=1, tiled=True),
    )
    part_router = (router_weight * router_gain[:, None]).astype(jnp.bfloat16)
    row_router = lax.all_gather(part_router, "rows", axis=0, tiled=True)
    serve_router = lax.all_gather(row_router, "owner", axis=1, tiled=True)
    return (serve_gate, serve_up, scale_gate, scale_up, serve_router)


def solution(mesh):
    placed = (
        P("owner", "rows", None),
        P("owner", "rows", None),
        P("owner", "rows", None),
        P("owner", "rows", None),
        P("owner"),
        P("rows", "owner"),
        P("rows"),
    )
    return jax.shard_map(
        shards,
        mesh=mesh,
        in_specs=placed,
        out_specs=(
            P("owner", None, None),
            P("owner", None, None),
            P("owner", None),
            P("owner", None),
            P(),
        ),
        check_vma=False,
    )
```

profile of v0, /device:TPU:0, one launch (start us, length us, event | category | flops | bytes accessed | tf_op | source)
XLA Modules:
  0.0 499.9 jit_solution(627092504670110036)
XLA Ops:
  7.2 0.0 all-gather.4.cloned.1.call-start
  7.2 0.7 broadcast_subtract_fusion
  7.9 0.0 copy-start.5
  7.9 22.6 %multiply_reduce_fusion = (f32[4,1024]{1,0:T(4,128)S(1)}, f32[4,1024]{1,0:T(4,128)S(1)}) fusion(f32[4,1024,1024]{2,1,0:T(8,128)} %param.10, f32[4]{0:T(128)S(1)} %broadcast_subtract_fusion, f32[4,1024,1024]{2,1,0:T(8,128)} %param.9, f32[4]{0:T(128)} %param.11, f32[4,1024,1024]{2,1,0:T(8,128)} %param.8, f32[4,1024,1024]{2,1,0:T(8,128)} %param.7), kind=kLoop, calls=%fused_computation.1 | loop fusion | flops 41934848 | bytes 67141664 | tf_op jit(solution)/shard_map/reduce_sum | solution.py:11
  30.5 9.9 %all-reduce = (f32[4,1024]{1,0:T(4,128)S(1)}, f32[4,1024]{1,0:T(4,128)S(1)}) all-reduce(f32[4,1024]{1,0:T(4,128)S(1)} %get-tuple-element.6, f32[4,1024]{1,0:T(4,128)S(1)} %get-tuple-element.5), channel_id=1, replica_groups=mesh['owner'=16,'rows'=2] {'rows'}, use_global_device_ids=true, to_apply=%region_1.0 | all-reduce | flops 8192 | bytes 65536 | tf_op jit(solution)/shard_map/psum | solution.py:10
  40.5 0.0 copy-start.1
  40.5 0.0 copy-done.5
  40.5 0.0 copy-start.2
  40.5 29.3 %divide_convert_fusion = (bf16[4,1024,1024]{2,1,0:T(8,128)(2,1)}, bf16[4,1024,1024]{2,1,0:T(8,128)(2,1)}) fusion(f32[4,1024]{1,0:T(4,128)S(1)} %sqrt.7, f32[4,1024,1024]{2,1,0:T(8,128)} %param.10, f32[4]{0:T(128)S(1)} %broadcast_subtract_fusion, f32[4,1024,1024]{2,1,0:T(8,128)} %param.9, f32[4]{0:T(128)S(1)} %copy-done.5, f32[4,1024]{1,0:T(4,128)S(1)} %sqrt.6, ...), kind=kLoop, calls=%fused_computation | loop fusion | flops 41943040 | bytes 83918880 | tf_op jit(solution)/shard_map/convert_element_type | solution.py:17
  69.8 0.0 copy-done.1
  69.8 0.0 copy-done.2
  69.8 0.0 copy-start.3
  69.9 0.0 copy-start.4
  69.9 0.0 all-gather.4.cloned.1.call-update
  69.9 0.0 all-gather.6.cloned.1.call-start
  69.9 0.7 all-gather.6.cloned.1.call-update
  70.6 0.0 copy-done.3
  70.7 0.0 copy-done.4
  70.7 4.4 all_gather.14
  75.0 22.2 %all-gather = bf16[16,4,2048]{2,1,0:T(4,128)(2,1)S(1)} all-gather(bf16[1,4,2048]{2,1,0:T(4,128)(2,1)S(1)} %bitcast.5), channel_id=1, replica_groups=mesh['owner'=16,'rows'=2] {'owner'}, dimensions={0}, use_global_device_ids=true | all-gather | bytes 278528 | tf_op jit(solution)/shard_map/all_gather | solution.py:25
  97.3 0.8 reshape.17
  98.0 171.1 %all-gather.4.cloned.1.call-done = bf16[4,2048,1024]{2,1,0:T(8,128)(2,1)} async-done(((bf16[4,1024,1024]{2,1,0:T(8,128)(2,1)}), bf16[4,2048,1024]{2,1,0:T(8,128)(2,1)}) %all-gather.4.cloned.1.call-update) | async-done | bytes 16777232 | tf_op jit(solution)/shard_map/all_gather | solution.py:20
  269.1 201.0 %all-gather.6.cloned.1.call-done = bf16[4,2048,1024]{2,1,0:T(8,128)(2,1)} async-done(((bf16[4,1024,1024]{2,1,0:T(8,128)(2,1)}), bf16[4,2048,1024]{2,1,0:T(8,128)(2,1)}) %all-gather.6.cloned.1.call-update) | async-done | bytes 16777232 | tf_op jit(solution)/shard_map/all_gather | solution.py:21
  470.1 0.0 copy-start
  470.1 14.8 %copy.14 = bf16[4,2048,1024]{2,1,0:T(8,128)(2,1)} copy(bf16[4,2048,1024]{2,1,0:T(8,128)(2,1)} %all-gather.4.cloned.1.call-done) | data formatting | bytes 33554432
  484.8 2.1 copy-done
  486.9 6.2 %copy.15 = bf16[4,2048,1024]{2,1,0:T(8,128)(2,1)} copy(bf16[4,2048,1024]{2,1,0:T(8,128)(2,1)S(1)} %copy-done) | data formatting | bytes 33554432
  (3 shorter events, 0.0 us)
Async XLA Ops:
  7.2 261.9 %all-gather.4.cloned.1.call-start = ((), (), s32[]{:S(2)}) async-start(), calls=%async_computation | async-start | bytes 25165824 | tf_op jit(solution)/shard_map/all_gather | solution.py:20
  7.9 32.6 %copy-start.5 = (f32[4]{0:T(128)S(1)}, f32[4]{0:T(128)}, u32[]{:S(2)}) copy-start(f32[4]{0:T(128)} %param.11) | copy-start | bytes 52
  40.5 29.4 %copy-start.1 = (f32[4,1024]{1,0:T(4,128)}, f32[4,1024]{1,0:T(4,128)S(1)}, u32[]{:S(2)}) copy-start(f32[4,1024]{1,0:T(4,128)S(1)} %sqrt.6) | copy-start | bytes 49156
  40.5 29.3 %copy-start.2 = (f32[4,1024]{1,0:T(4,128)}, f32[4,1024]{1,0:T(4,128)S(1)}, u32[]{:S(2)}) copy-start(f32[4,1024]{1,0:T(4,128)S(1)} %sqrt.7) | copy-start | bytes 49156
  69.8 0.8 copy-start.3
  69.9 0.8 copy-start.4
  69.9 400.2 %all-gather.6.cloned.1.call-start = ((), (), s32[]{:S(2)}) async-start(), calls=%async_computation.1 | async-start | bytes 25165824 | tf_op jit(solution)/shard_map/all_gather | solution.py:21
  470.1 16.9 %copy-start = (bf16[4,2048,1024]{2,1,0:T(8,128)(2,1)S(1)}, bf16[4,2048,1024]{2,1,0:T(8,128)(2,1)}, u32[]{:S(2)}) copy-start(bf16[4,2048,1024]{2,1,0:T(8,128)(2,1)} %all-gather.6.cloned.1.call-done) | copy-start | bytes 50331652
Sparse Core Ops, SparseCore 0:
  70.0 199.0 all-gather.3
  271.2 198.8 all-gather.5
where the time goes:
time: 500 us
  waiting for transfers between devices  373 us (75%)
  other arithmetic  52.6 us (11%)
  blocking collectives  36.5 us (7%)
  local copies, waits for them, and re-layouts  23.9 us (5%)
  between operations  14.1 us (3%)
    all_gather x1, waiting for transfers between devices, shards(): lax.all_gather(narrow_up, 'rows', axis=1, tiled=True)  201 us
    all_gather x1, waiting for transfers between devices, shards(): lax.all_gather(narrow_gate, 'rows', axis=1, tiled=True)  171 us
    convert_element_type x1, other arithmetic, shards(): (fresh_up / jnp.expand_dims(scale_up, 1)).astype(jnp.bfloat16)  29.3 us
    unnamed x15, local copies, waits for them, and re-layouts  23.8 us
    reduce_sum x1, other arithmetic, shards(): jnp.sum(fresh_up * fresh_up, axis=1)  22.6 us
    all_gather x1, blocking collectives, shards(): serve_router = lax.all_gather(row_router, 'owner', axis=1, tiled=True)  22.2 us
  transfers between devices with their start and end apart: 2, of which 2 were waited for; matrix products, arithmetic and copies ran while one was open for 0% of the time, Pallas kernels for 0%

commit v1 on v0

v1 whole, which is shorter than its diff:
```python
import functools
import math

import jax
import jax.numpy as jnp
from jax import lax
from jax.experimental import pallas as pl
from jax.experimental.pallas import tpu as pltpu
from jax.sharding import PartitionSpec as P


ANY = pl.BlockSpec(memory_space=pl.ANY)
SMEM = pl.BlockSpec(memory_space=pltpu.SMEM)


def shift(x, n, k):
    return lax.ppermute(x, "rows", [((j + k) % n, j) for j in range(n)])


def halves_of(part, n):
    if n == 2:
        return part, shift(part, n, 1)
    if n == 1:
        return part, jnp.zeros_like(part)
    me = lax.axis_index("rows")
    stacked = jnp.stack([part] + [shift(part, n, k) for k in range(1, n)])
    total = jnp.zeros_like(part)
    for j in range(n):
        total = total + lax.dynamic_index_in_dim(stacked, lax.rem(j - me + n, n), 0, keepdims=False)
    return total, jnp.zeros_like(part)


def sum_kernel(first, share_ref, w_ref, avg_ref, dep_ref, out_ref):
    share = share_ref[pl.program_id(0) + first]
    fresh = share * w_ref[0] + (1.0 - share) * avg_ref[0]
    part = jnp.sum(fresh * fresh, axis=0, keepdims=True)[None]

    @pl.when(pl.program_id(1) == 0)
    def _():
        out_ref[...] = part

    @pl.when(pl.program_id(1) != 0)
    def _():
        out_ref[...] += part


def sums(share, w, avg, first, count, tile, dep):
    _, depth, width = w.shape
    spec = pl.BlockSpec((1, tile, width), lambda e, t: (e + first, t, 0))
    return pl.pallas_call(
        functools.partial(sum_kernel, first),
        grid=(count, depth // tile),
        in_specs=[SMEM, spec, spec, ANY],
        out_specs=pl.BlockSpec((1, 1, width), lambda e, t: (e, 0, 0)),
        out_shape=jax.ShapeDtypeStruct((count, 1, width), jnp.float32),
        cost_estimate=pl.CostEstimate(
            flops=5 * count * depth * width, bytes_accessed=8 * count * depth * width, transcendentals=0
        ),
    )(share, w, avg, dep)


def narrow_kernel(e, me_ref, share_ref, w_ref, avg_ref, a_ref, b_ref, *refs):
    send_ref, scale_ref, out_ref = refs[-3:]
    share = share_ref[e]
    fresh = share * w_ref[0] + (1.0 - share) * avg_ref[0]
    scale = jnp.sqrt(a_ref[0] + b_ref[0])
    served = (fresh / scale).astype(jnp.bfloat16)
    scale_ref[...] = scale
    send_ref[...] = served
    out_ref[0] = served


def narrow(me, share, w, avg, a, b, at, e, column, columns, n, tile, out, dep):
    experts, depth, width = w.shape
    tiles = depth // tile
    spec = pl.BlockSpec((1, tile, columns), lambda t, me: (e, t, column))
    sum_spec = pl.BlockSpec((1, 1, columns), lambda t, me: (at, 0, column))
    args = [share, w, avg, a, b, dep]
    in_specs = [SMEM, spec, spec, sum_spec, sum_spec, ANY]
    aliases = {}
    if out is not None:
        args.append(out)
        in_specs.append(ANY)
        aliases = {len(args): 2}
    return pl.pallas_call(
        functools.partial(narrow_kernel, e),
        grid_spec=pltpu.PrefetchScalarGridSpec(
            num_scalar_prefetch=1,
            grid=(tiles,),
            in_specs=in_specs,
            out_specs=[
                pl.BlockSpec((tile, columns), lambda t, me: (t, 0)),
                pl.BlockSpec((1, columns), lambda t, me: (0, 0)),
                pl.BlockSpec((1, tile, columns), lambda t, me: (e, me[0] * tiles + t, column)),
            ],
        ),
        out_shape=[
            jax.ShapeDtypeStruct((depth, columns), jnp.bfloat16),
            jax.ShapeDtypeStruct((1, columns), jnp.float32),
            jax.ShapeDtypeStruct((experts, n * depth, width), jnp.bfloat16),
        ],
        input_output_aliases=aliases,
        cost_estimate=pl.CostEstimate(
            flops=8 * depth * columns, bytes_accessed=12 * depth * columns, transcendentals=0
        ),
    )(me, *args)


def router_kernel(weight_ref, gain_ref, dep_ref, out_ref):
    out_ref[...] = (weight_ref[...] * gain_ref[...]).astype(jnp.bfloat16)


def router_part(weight, gain, dep):
    return pl.pallas_call(
        router_kernel,
        in_specs=[pl.BlockSpec(), pl.BlockSpec(), ANY],
        out_shape=jax.ShapeDtypeStruct(weight.shape, jnp.bfloat16),
        cost_estimate=pl.CostEstimate(flops=weight.size, bytes_accessed=8 * weight.size, transcendentals=0),
    )(weight, gain, dep)


def later_kernel(x_ref, dep_ref, out_ref):
    out_ref[...] = x_ref[...]


def later(x, dep):
    return pl.pallas_call(
        later_kernel,
        in_specs=[pl.BlockSpec(), ANY],
        out_shape=jax.ShapeDtypeStruct(x.shape, x.dtype),
        cost_estimate=pl.CostEstimate(flops=0, bytes_accessed=4 * x.size, transcendentals=0),
    )(x, dep)


def make_shards(n):
    def shards(w_gate, avg_gate, w_up, avg_up, mix_share, router_weight, router_gain):
        me = lax.axis_index("rows").astype(jnp.int32)
        at = me[None]
        experts, depth, width = w_gate.shape
        pairs = ((w_gate, avg_gate), (w_up, avg_up))
        tile = math.gcd(depth, 256)
        half = width // 2

        pieces = [(0, 0, 0, half), (0, 0, 1, half)]
        middle = [(which, e) for e in range(experts) for which in range(2)][1:]
        for which, e in middle[:-1]:
            pieces.append((which, e, 0, width))
        pieces += [(*middle[-1], 0, half), (*middle[-1], 1, half)]

        outs, scales, sends = [None, None], {}, []

        def send_piece(piece, halves, row, dep):
            which, e, column, columns = piece
            w, avg = pairs[which]
            send, scale, outs[which] = narrow(
                at, mix_share, w, avg, *halves, row, e, column, columns, n, tile, outs[which], dep
            )
            scales.setdefault((which, e), []).append(scale)
            sends.append((piece, [shift(send, n, k) for k in range(1, n)]))
            return send

        part = sums(mix_share, *pairs[0], 0, 1, tile, mix_share)
        router = router_part(router_weight.T, router_gain[None], part)
        halves = halves_of(part, n)
        sent = send_piece(pieces[0], halves, 0, part)

        held = {}
        last = sent
        if experts > 1:
            last = sums(mix_share, *pairs[0], 1, experts - 1, tile, last)
            held[0] = halves_of(last, n)
        last = sums(mix_share, *pairs[1], 0, experts, tile, last)
        held[1] = halves_of(last, n)

        last = send_piece(pieces[1], halves, 0, last)
        for piece in pieces[2:]:
            which, e = piece[:2]
            last = send_piece(piece, held[which], e if which else e - 1, last)

        moved = [shift(router, n, k) for k in range(1, n)]
        row_router = jnp.zeros((router.shape[0], n * depth), jnp.bfloat16)
        row_router = lax.dynamic_update_slice(row_router, router, (0, me * depth))
        for k in range(1, n):
            row_router = lax.dynamic_update_slice(
                row_router, moved[k - 1], (0, lax.rem(me + k, n) * depth)
            )
        serve_router = lax.all_gather(later(row_router, last), "owner", axis=0, tiled=True).T

        for (which, e, column, columns), got in sends:
            for k in range(1, n):
                outs[which] = lax.dynamic_update_slice(
                    outs[which], got[k - 1][None], (e, lax.rem(me + k, n) * depth, column * columns)
                )

        scale_gate, scale_up = (
            jnp.concatenate([jnp.concatenate(scales[which, e], axis=1) for e in range(experts)], axis=0)
            for which in range(2)
        )
        return (outs[0], outs[1], scale_gate, scale_up, serve_router)

    return shards


def solution(mesh):
    placed = (
        P("owner", "rows", None),
        P("owner", "rows", None),
        P("owner", "rows", None),
        P("owner", "rows", None),
        P("owner"),
        P("rows", "owner"),
        P("rows"),
    )
    return jax.shard_map(
        make_shards(mesh.shape["rows"]),
        mesh=mesh,
        in_specs=placed,
        out_specs=(
            P("owner", None, None),
            P("owner", None, None),
            P("owner", None),
            P("owner", None),
            P(),
        ),
        check_vma=False,
    )
```

time: 500 us -> 423 us (0.85)
  waiting for transfers between devices: 373 us -> 263 us
  Pallas kernels: 0 us -> 91.3 us
  other arithmetic: 52.6 us -> 1.93 us
  starting transfers between devices: 0.08 us -> 17.1 us
  blocking collectives: 36.5 us -> 22.8 us
  between operations: 14.1 us -> 0.78 us
    all_gather x2 -> x0, waiting for transfers between devices: 372 us -> none  [the longest x1 201 us: shards(): lax.all_gather(narrow_up, 'rows', axis=1, tiled=True)]
    ppermute x0 -> x14, waiting for transfers between devices: none -> 263 us  [shift(): return lax.ppermute(x, 'rows', [((j + k) % n, j) for j in range(n)])]
    pallas_call x0 -> x15, Pallas kernels: none -> 91.3 us  [the longest x10 52.7 us: narrow(): pl.pallas_call(functools.partial(narrow_kernel, e), grid_spec=pltpu.Prefe...]
    convert_element_type x2 -> x0, other arithmetic: 29.3 us -> none  [the longest x1 29.3 us: shards(): (fresh_up / jnp.expand_dims(scale_up, 1)).astype(jnp.bfloat16)]
    reduce_sum x1 -> x0, other arithmetic: 22.6 us -> none  [shards(): jnp.sum(fresh_up * fresh_up, axis=1)]
    dynamic_update_slice x0 -> x12, local copies, waits for them, and re-layouts: none -> 21.9 us  [the longest x10 21.9 us: shards(): lax.dynamic_update_slice(outs[which], got[k - 1][None], (e, lax.rem(me +...]
    unnamed x15 -> x35, local copies, waits for them, and re-layouts: 23.8 us -> 2.62 us
    ppermute x0 -> x14, starting transfers between devices: none -> 17.1 us  [shift(): return lax.ppermute(x, 'rows', [((j + k) % n, j) for j in range(n)])]
  transfers between devices with their start and end apart: 2 -> 14, of which waited for: 2 -> 4; matrix products, arithmetic and copies ran while one was open for 0% -> 6% of each run, Pallas kernels for 0% -> 12%
where the time goes in v1:
time: 423 us; the launch traced here: 421 us
  waiting for transfers between devices  263 us (62%)
  Pallas kernels  91.3 us (22%)
  local copies, waits for them, and re-layouts  24.6 us (6%)
  blocking collectives  22.8 us (5%)
  starting transfers between devices  17.1 us (4%)
    ppermute x14, waiting for transfers between devices, shift(): return lax.ppermute(x, 'rows', [((j + k) % n, j) for j in range(n)])  263 us
    pallas_call x10, Pallas kernels, narrow(): pl.pallas_call(functools.partial(narrow_kernel, e), grid_spec=pltpu.Prefe...  52.7 us
    pallas_call x3, Pallas kernels, sums(): pl.pallas_call(functools.partial(sum_kernel, first), grid=(count, depth /...  36 us
    all_gather x1, blocking collectives, shards(): lax.all_gather(later(row_router, last), 'owner', axis=0, tiled=True)  22.8 us
    dynamic_update_slice x10, local copies, waits for them, and re-layouts, shards(): lax.dynamic_update_slice(outs[which], got[k - 1][None], (e, lax.rem(me +...  21.9 us
    ppermute x14, starting transfers between devices, shift(): return lax.ppermute(x, 'rows', [((j + k) % n, j) for j in range(n)])  17.1 us
  transfers between devices with their start and end apart: 14, of which 4 were waited for; matrix products, arithmetic and copies ran while one was open for 6% of the time, Pallas kernels for 12%

profile of v1, /device:TPU:0, one launch (start us, length us, event | category | flops | bytes accessed | tf_op | source)
XLA Modules:
  0.0 421.5 jit_solution(15354757997400307987)
XLA Ops:
  0.6 5.1 %shard_map.110.a_ref.refs_0_.dep_ref = f32[1,1,1024]{2,1,0:T(1,128)} custom-call(f32[4]{0:T(128)} %share_ref.25, f32[4,1024,1024]{2,1,0:T(8,128)} %w_ref.23, f32[4,1024,1024]{2,1,0:T(8,128)} %avg_ref.23, f32[4]{0:T(128)} %share_ref.25), custom_call_target="tpu_custom_call" | custom-call | flops 5242880 | bytes 8388608 | tf_op jit(solution)/shard_map/pallas_call | solution.py:50
  5.8 3.0 collective-permute-start
  8.7 1.8 collective-permute-done.b_ref
  10.5 0.6 copy-done.7
  11.1 4.2 %shard_map.111 = (bf16[1024,512]{1,0:T(8,128)(2,1)}, f32[1,512]{1,0:T(1,128)}, bf16[4,2048,1024]{2,1,0:T(8,128)(2,1)}) custom-call(s32[1]{0:T(128)} %bitcast.me_ref, f32[4]{0:T(128)} %share_ref.25, f32[4,1024,1024]{2,1,0:T(8,128)} %w_ref.23, f32[4,1024,1024]{2,1,0:T(8,128)} %avg_ref.23, f32[1,1,1024]{2,1,0:T(1,128)} %shard_map.110.a_ref.refs_0_.dep_ref, ...), custom_call_target="tpu_custom_call" | custom-call | flops 4194304 | bytes 6291456 | tf_op jit(solution)/shard_map/pallas_call | solution.py:85
  15.4 13.4 %shard_map.112.dep_ref.a_ref = f32[3,1,1024]{2,1,0:T(1,128)} custom-call(f32[4]{0:T(128)} %share_ref.25, f32[4,1024,1024]{2,1,0:T(8,128)} %w_ref.23, f32[4,1024,1024]{2,1,0:T(8,128)} %avg_ref.23, bf16[1024,512]{1,0:T(8,128)(2,1)} %get-tuple-element.35.dep_ref), custom_call_target="tpu_custom_call" | custom-call | flops 15728640 | bytes 25165824 | tf_op jit(solution)/shard_map/pallas_call | solution.py:50
  28.7 17.5 %shard_map.113.refs_0_.a_ref = f32[4,1,1024]{2,1,0:T(1,128)} custom-call(f32[4]{0:T(128)} %share_ref.25, f32[4,1024,1024]{2,1,0:T(8,128)} %w_ref.25, f32[4,1024,1024]{2,1,0:T(8,128)} %avg_ref.25, f32[3,1,1024]{2,1,0:T(1,128)} %shard_map.112.dep_ref.a_ref), custom_call_target="tpu_custom_call" | custom-call | flops 20971520 | bytes 33554432 | tf_op jit(solution)/shard_map/pallas_call | solution.py:50
  46.2 2.0 collective-permute-start.2
  48.2 0.1 collective-permute-start.1
  48.3 4.2 %shard_map.114 = (bf16[1024,512]{1,0:T(8,128)(2,1)}, f32[1,512]{1,0:T(1,128)}, bf16[4,2048,1024]{2,1,0:T(8,128)(2,1)}) custom-call(s32[1]{0:T(128)} %bitcast.me_ref, f32[4]{0:T(128)} %share_ref.25, f32[4,1024,1024]{2,1,0:T(8,128)} %w_ref.23, f32[4,1024,1024]{2,1,0:T(8,128)} %avg_ref.23, ...), custom_call_target="tpu_custom_call", output_to_operand_aliasing={{2}: (7, {})} | custom-call | flops 4194304 | bytes 6291456 | tf_op jit(solution)/shard_map/pallas_call | solution.py:85
  52.6 0.0 collective-permute-done.2.b_ref
  52.6 0.0 copy-start.2
  52.6 0.6 copy-done.2
  53.2 5.9 %shard_map.115 = (bf16[1024,1024]{1,0:T(8,128)(2,1)}, f32[1,1024]{1,0:T(1,128)}, bf16[4,2048,1024]{2,1,0:T(8,128)(2,1)}) custom-call(s32[1]{0:T(128)} %bitcast.me_ref, f32[4]{0:T(128)} %share_ref.25, f32[4,1024,1024]{2,1,0:T(8,128)} %w_ref.25, f32[4,1024,1024]{2,1,0:T(8,128)} %avg_ref.25, f32[4,1,1024]{2,1,0:T(1,128)} %shard_map.113.refs_0_.a_ref, ...), custom_call_target="tpu_custom_call" | custom-call | flops 8388608 | bytes 12582912 | tf_op jit(solution)/shard_map/pallas_call | solution.py:85
  59.1 2.0 collective-permute-start.8
  61.0 0.0 collective-permute-done.1.b_ref
  61.0 0.6 copy-done.4
  61.6 5.9 %shard_map.116 = (bf16[1024,1024]{1,0:T(8,128)(2,1)}, f32[1,1024]{1,0:T(1,128)}, bf16[4,2048,1024]{2,1,0:T(8,128)(2,1)}) custom-call(s32[1]{0:T(128)} %bitcast.me_ref, f32[4]{0:T(128)} %share_ref.25, f32[4,1024,1024]{2,1,0:T(8,128)} %w_ref.23, f32[4,1024,1024]{2,1,0:T(8,128)} %avg_ref.23, ...), custom_call_target="tpu_custom_call", output_to_operand_aliasing={{2}: (7, {})} | custom-call | flops 8388608 | bytes 12582912 | tf_op jit(solution)/shard_map/pallas_call | solution.py:85
  67.5 6.0 %shard_map.117 = (bf16[1024,1024]{1,0:T(8,128)(2,1)}, f32[1,1024]{1,0:T(1,128)}, bf16[4,2048,1024]{2,1,0:T(8,128)(2,1)}) custom-call(s32[1]{0:T(128)} %bitcast.me_ref, f32[4]{0:T(128)} %share_ref.25, f32[4,1024,1024]{2,1,0:T(8,128)} %w_ref.25, f32[4,1024,1024]{2,1,0:T(8,128)} %avg_ref.25, ...), custom_call_target="tpu_custom_call", output_to_operand_aliasing={{2}: (7, {})} | custom-call | flops 8388608 | bytes 12582912 | tf_op jit(solution)/shard_map/pallas_call | solution.py:85
  73.5 0.1 collective-permute-start.9
  73.6 2.0 collective-permute-start.3
  75.5 0.1 collective-permute-start.4
  75.6 1.3 shard_map.123
  76.9 2.0 collective-permute-start.13
  78.9 5.9 %shard_map.118 = (bf16[1024,1024]{1,0:T(8,128)(2,1)}, f32[1,1024]{1,0:T(1,128)}, bf16[4,2048,1024]{2,1,0:T(8,128)(2,1)}) custom-call(s32[1]{0:T(128)} %bitcast.me_ref, f32[4]{0:T(128)} %share_ref.25, f32[4,1024,1024]{2,1,0:T(8,128)} %w_ref.23, f32[4,1024,1024]{2,1,0:T(8,128)} %avg_ref.23, ...), custom_call_target="tpu_custom_call", output_to_operand_aliasing={{2}: (7, {})} | custom-call | flops 8388608 | bytes 12582912 | tf_op jit(solution)/shard_map/pallas_call | solution.py:85
  84.8 5.9 %shard_map.119 = (bf16[1024,1024]{1,0:T(8,128)(2,1)}, f32[1,1024]{1,0:T(1,128)}, bf16[4,2048,1024]{2,1,0:T(8,128)(2,1)}) custom-call(s32[1]{0:T(128)} %bitcast.me_ref, f32[4]{0:T(128)} %share_ref.25, f32[4,1024,1024]{2,1,0:T(8,128)} %w_ref.25, f32[4,1024,1024]{2,1,0:T(8,128)} %avg_ref.25, ...), custom_call_target="tpu_custom_call", output_to_operand_aliasing={{2}: (7, {})} | custom-call | flops 8388608 | bytes 12582912 | tf_op jit(solution)/shard_map/pallas_call | solution.py:85
  90.7 104.6 %collective-permute-done.13 = bf16[4,1024]{1,0:T(4,128)(2,1)S(1)} collective-permute-done((bf16[4,1024]{1,0:T(4,128)(2,1)}, bf16[4,1024]{1,0:T(4,128)(2,1)S(1)}, u32[]{:S(2)}, u32[]{:S(2)}) %collective-permute-start.13) | collective-permute-done | bytes 8224 | tf_op jit(solution)/shard_map/ppermute | solution.py:17
  195.3 1.7 collective-permute-start.10
  197.0 0.0 copy-start.5
  197.0 5.9 %shard_map.120 = (bf16[1024,1024]{1,0:T(8,128)(2,1)}, f32[1,1024]{1,0:T(1,128)}, bf16[4,2048,1024]{2,1,0:T(8,128)(2,1)}) custom-call(s32[1]{0:T(128)} %bitcast.me_ref, f32[4]{0:T(128)} %share_ref.25, f32[4,1024,1024]{2,1,0:T(8,128)} %w_ref.23, f32[4,1024,1024]{2,1,0:T(8,128)} %avg_ref.23, ...), custom_call_target="tpu_custom_call", output_to_operand_aliasing={{2}: (7, {})} | custom-call | flops 8388608 | bytes 12582912 | tf_op jit(solution)/shard_map/pallas_call | solution.py:85
  203.0 4.3 %shard_map.121 = (bf16[1024,512]{1,0:T(8,128)(2,1)}, f32[1,512]{1,0:T(1,128)}, bf16[4,2048,1024]{2,1,0:T(8,128)(2,1)}) custom-call(s32[1]{0:T(128)} %bitcast.me_ref, f32[4]{0:T(128)} %share_ref.25, f32[4,1024,1024]{2,1,0:T(8,128)} %w_ref.25, f32[4,1024,1024]{2,1,0:T(8,128)} %avg_ref.25, ...), custom_call_target="tpu_custom_call", output_to_operand_aliasing={{2}: (7, {})} | custom-call | flops 4194304 | bytes 6291456 | tf_op jit(solution)/shard_map/pallas_call | solution.py:85
  207.3 4.4 %shard_map.122 = (bf16[1024,512]{1,0:T(8,128)(2,1)}, f32[1,512]{1,0:T(1,128)}, bf16[4,2048,1024]{2,1,0:T(8,128)(2,1)}) custom-call(s32[1]{0:T(128)} %bitcast.me_ref, f32[4]{0:T(128)} %share_ref.25, f32[4,1024,1024]{2,1,0:T(8,128)} %w_ref.25, f32[4,1024,1024]{2,1,0:T(8,128)} %avg_ref.25, ...), custom_call_target="tpu_custom_call", output_to_operand_aliasing={{2}: (7, {})} | custom-call | flops 4194304 | bytes 6291456 | tf_op jit(solution)/shard_map/pallas_call | solution.py:85
  211.7 1.3 shard_map.124
  213.1 0.0 collective-permute-done.3
  213.1 0.4 collective-permute-start.5
  213.4 22.8 %all-gather = bf16[16,4,2048]{2,1,0:T(4,128)(2,1)S(1)} all-gather(bf16[1,4,2048]{2,1,0:T(4,128)(2,1)} %bitcast.26), channel_id=1, replica_groups=mesh['owner'=16,'rows'=2] {'owner'}, dimensions={0}, use_global_device_ids=true | all-gather | bytes 278528 | tf_op jit(solution)/shard_map/all_gather | solution.py:187
  236.2 0.8 reshape.11
  236.9 0.0 copy-done.10
  237.0 0.0 copy-done.13
  237.0 0.6 pad_maximum_fusion
  237.6 1.3 maximum_maximum_fusion
  238.9 0.0 collective-permute-done.4
  238.9 1.5 collective-permute-start.6
  240.4 2.3 bitcast_dynamic-update-slice_fusion.9
  242.7 0.0 collective-permute-done.8
  242.7 0.5 collective-permute-start.7
  243.2 0.0 collective-permute-done.9
  243.2 1.5 collective-permute-start.11
  244.7 2.3 bitcast_dynamic-update-slice_fusion.8
  247.0 3.1 bitcast_dynamic-update-slice_fusion.2
  250.0 3.1 bitcast_dynamic-update-slice_fusion.1
  253.1 0.0 collective-permute-done.10
  253.1 0.5 collective-permute-start.12
  253.7 3.1 bitcast_dynamic-update-slice_fusion
  256.7 144.5 %collective-permute-done.11 = bf16[1024,512]{1,0:T(8,128)(2,1)S(1)} collective-permute-done((bf16[1024,512]{1,0:T(8,128)(2,1)}, bf16[1024,512]{1,0:T(8,128)(2,1)S(1)}, u32[]{:S(2)}, u32[]{:S(2)}) %collective-permute-start.11) | collective-permute-done | bytes 1048608 | tf_op jit(solution)/shard_map/ppermute | solution.py:17
  401.3 1.0 bitcast_dynamic-update-slice_fusion.7
  402.3 0.0 collective-permute-done.5
  402.3 3.1 bitcast_dynamic-update-slice_fusion.5
  405.4 0.0 collective-permute-done.6
  405.4 1.5 bitcast_dynamic-update-slice_fusion.4
  406.9 0.0 collective-permute-done.7
  406.9 1.5 bitcast_dynamic-update-slice_fusion.3
  408.4 12.0 %collective-permute-done.12 = bf16[1024,512]{1,0:T(8,128)(2,1)S(1)} collective-permute-done((bf16[1024,512]{1,0:T(8,128)(2,1)}, bf16[1024,512]{1,0:T(8,128)(2,1)S(1)}, u32[]{:S(2)}, u32[]{:S(2)}) %collective-permute-start.12) | collective-permute-done | bytes 1048608 | tf_op jit(solution)/shard_map/ppermute | solution.py:17
  420.4 1.0 bitcast_dynamic-update-slice_fusion.6
  (30 shorter events, 0.1 us)
Async XLA Ops:
  5.8 4.8 %collective-permute-start = (f32[1,1,1024]{2,1,0:T(1,128)}, f32[1,1,1024]{2,1,0:T(1,128)S(1)}, u32[]{:S(2)}, u32[]{:S(2)}) collective-permute-start(f32[1,1,1024]{2,1,0:T(1,128)} %shard_map.110.a_ref.refs_0_.dep_ref), channel_id=1, source_target_pairs={{1,0},{0,1},{3,2},{2,3},{5,4},{4,5},{7,6},{6,7},{9,8},{8,9},{11,10... | collective-permute-start | bytes 12296 | tf_op jit(solution)/shard_map/ppermute | solution.py:17
  10.5 0.6 copy-start.7
  28.7 19.5 %copy-start.3 = (f32[3,1,1024]{2,1,0:T(1,128)S(1)}, f32[3,1,1024]{2,1,0:T(1,128)}, u32[]{:S(2)}) copy-start(f32[3,1,1024]{2,1,0:T(1,128)} %shard_map.112.dep_ref.a_ref) | copy-start | bytes 36868
  46.2 6.3 %collective-permute-start.2 = (f32[4,1,1024]{2,1,0:T(1,128)}, f32[4,1,1024]{2,1,0:T(1,128)S(1)}, u32[]{:S(2)}, u32[]{:S(2)}) collective-permute-start(f32[4,1,1024]{2,1,0:T(1,128)} %shard_map.113.refs_0_.a_ref), channel_id=1, source_target_pairs={{1,0},{0,1},{3,2},{2,3},{5,4},{4,5},{7,6},{6,7},{9,8},{8,9},{11,10... | collective-permute-start | bytes 49160 | tf_op jit(solution)/shard_map/ppermute | solution.py:17
  48.2 12.8 %collective-permute-start.1 = (f32[3,1,1024]{2,1,0:T(1,128)S(1)}, f32[3,1,1024]{2,1,0:T(1,128)S(1)}, u32[]{:S(2)}, u32[]{:S(2)}) collective-permute-start(f32[3,1,1024]{2,1,0:T(1,128)S(1)} %copy-done.3), channel_id=1, source_target_pairs={{1,0},{0,1},{3,2},{2,3},{5,4},{4,5},{7,6},{6,7},{9,8},{8,9},{11,10... | collective-permute-start | bytes 36872 | tf_op jit(solution)/shard_map/ppermute | solution.py:17
  52.6 0.6 copy-start.2
  59.1 183.6 %collective-permute-start.8 = (bf16[1024,1024]{1,0:T(8,128)(2,1)}, bf16[1024,1024]{1,0:T(8,128)(2,1)}, u32[]{:S(2)}, u32[]{:S(2)}) collective-permute-start(bf16[1024,1024]{1,0:T(8,128)(2,1)} %get-tuple-element.38.refs_0_), channel_id=1, source_target_pairs={{1,0},{0,1},{3,2},{2,3},{5,4},{4,5},{7,6},{6,7},{9,8},{8,9},{11,10... | collective-permute-start | bytes 6291464 | tf_op jit(solution)/shard_map/ppermute | solution.py:17
  61.0 0.6 copy-start.4
  67.5 8.0 %copy-start.1 = (bf16[1024,512]{1,0:T(8,128)(2,1)S(1)}, bf16[1024,512]{1,0:T(8,128)(2,1)}, u32[]{:S(2)}) copy-start(bf16[1024,512]{1,0:T(8,128)(2,1)} %get-tuple-element.37.refs_0_) | copy-start | bytes 3145732
  73.5 169.7 %collective-permute-start.9 = (bf16[1024,1024]{1,0:T(8,128)(2,1)}, bf16[1024,1024]{1,0:T(8,128)(2,1)}, u32[]{:S(2)}, u32[]{:S(2)}) collective-permute-start(bf16[1024,1024]{1,0:T(8,128)(2,1)} %get-tuple-element.42.refs_0_), channel_id=1, source_target_pairs={{1,0},{0,1},{3,2},{2,3},{5,4},{4,5},{7,6},{6,7},{9,8},{8,9},{11,10... | collective-permute-start | bytes 6291464 | tf_op jit(solution)/shard_map/ppermute | solution.py:17
  73.6 139.5 %collective-permute-start.3 = (bf16[1024,512]{1,0:T(8,128)(2,1)}, bf16[1024,512]{1,0:T(8,128)(2,1)}, u32[]{:S(2)}, u32[]{:S(2)}) collective-permute-start(bf16[1024,512]{1,0:T(8,128)(2,1)} %get-tuple-element.35.dep_ref), channel_id=1, source_target_pairs={{1,0},{0,1},{3,2},{2,3},{5,4},{4,5},{7,6},{6,7},{9,8},{8,9},{11,10... | collective-permute-start | bytes 3145736 | tf_op jit(solution)/shard_map/ppermute | solution.py:17
  75.5 163.4 %collective-permute-start.4 = (bf16[1024,512]{1,0:T(8,128)(2,1)S(1)}, bf16[1024,512]{1,0:T(8,128)(2,1)}, u32[]{:S(2)}, u32[]{:S(2)}) collective-permute-start(bf16[1024,512]{1,0:T(8,128)(2,1)S(1)} %copy-done.1), channel_id=1, source_target_pairs={{1,0},{0,1},{3,2},{2,3},{5,4},{4,5},{7,6},{6,7},{9,8},{8,9},{11,10... | collective-permute-start | bytes 3145736 | tf_op jit(solution)/shard_map/ppermute | solution.py:17
  76.9 118.3 %collective-permute-start.13 = (bf16[4,1024]{1,0:T(4,128)(2,1)}, bf16[4,1024]{1,0:T(4,128)(2,1)S(1)}, u32[]{:S(2)}, u32[]{:S(2)}) collective-permute-start(bf16[4,1024]{1,0:T(4,128)(2,1)} %shard_map.123), channel_id=1, source_target_pairs={{1,0},{0,1},{3,2},{2,3},{5,4},{4,5},{7,6},{6,7},{9,8},{8,9},{11,10... | collective-permute-start | bytes 24584 | tf_op jit(solution)/shard_map/ppermute | solution.py:17
  84.8 112.2 %copy-start.6 = (bf16[4,1024]{1,0:T(4,128)(2,1)S(1)}, bf16[4,1024]{1,0:T(4,128)(2,1)}, u32[]{:S(2)}) copy-start(bf16[4,1024]{1,0:T(4,128)(2,1)} %shard_map.123) | copy-start | bytes 24580
  195.3 57.8 %collective-permute-start.10 = (bf16[1024,1024]{1,0:T(8,128)(2,1)}, bf16[1024,1024]{1,0:T(8,128)(2,1)}, u32[]{:S(2)}, u32[]{:S(2)}) collective-permute-start(bf16[1024,1024]{1,0:T(8,128)(2,1)} %get-tuple-element.46.refs_0_), channel_id=1, source_target_pairs={{1,0},{0,1},{3,2},{2,3},{5,4},{4,5},{7,6},{6,7},{9,8},{8,9},{11,10... | collective-permute-start | bytes 6291464 | tf_op jit(solution)/shard_map/ppermute | solution.py:17
  197.0 5.9 %copy-start.5 = (bf16[4,2048]{1,0:T(4,128)(2,1)}, bf16[4,2048]{1,0:T(4,128)(2,1)S(1)}, u32[]{:S(2)}) copy-start(bf16[4,2048]{1,0:T(4,128)(2,1)S(1)} %constant_dynamic-update-slice_fusion.x_ref) | copy-start | bytes 49156
  207.2 5.8 %copy-start = (bf16[1024,1024]{1,0:T(8,128)(2,1)S(1)}, bf16[1024,1024]{1,0:T(8,128)(2,1)}, u32[]{:S(2)}) copy-start(bf16[1024,1024]{1,0:T(8,128)(2,1)} %get-tuple-element.40.refs_0_) | copy-start | bytes 6291460
  207.2 29.7 %copy-start.10 = (f32[1,1024]{1,0:T(1,128)S(1)}, f32[1,1024]{1,0:T(1,128)}, u32[]{:S(2)}) copy-start(f32[1,1024]{1,0:T(1,128)} %get-tuple-element.57) | copy-start | bytes 12292
  207.2 29.7 %copy-start.12 = (f32[1,1024]{1,0:T(1,128)S(1)}, f32[1,1024]{1,0:T(1,128)}, u32[]{:S(2)}) copy-start(f32[1,1024]{1,0:T(1,128)} %get-tuple-element.58) | copy-start | bytes 12292
  207.3 29.7 %copy-start.13 = (f32[1,1024]{1,0:T(1,128)S(1)}, f32[1,1024]{1,0:T(1,128)}, u32[]{:S(2)}) copy-start(f32[1,1024]{1,0:T(1,128)} %get-tuple-element.59) | copy-start | bytes 12292
  207.3 29.7 %copy-start.14 = (f32[1,512]{1,0:T(1,128)S(1)}, f32[1,512]{1,0:T(1,128)}, u32[]{:S(2)}) copy-start(f32[1,512]{1,0:T(1,128)} %get-tuple-element.55) | copy-start | bytes 6148
  207.3 29.7 %copy-start.15 = (f32[1,512]{1,0:T(1,128)S(1)}, f32[1,512]{1,0:T(1,128)}, u32[]{:S(2)}) copy-start(f32[1,512]{1,0:T(1,128)} %get-tuple-element.56) | copy-start | bytes 6148
  207.3 30.3 %copy-start.8 = (f32[1,1024]{1,0:T(1,128)S(1)}, f32[1,1024]{1,0:T(1,128)}, u32[]{:S(2)}) copy-start(f32[1,1024]{1,0:T(1,128)} %get-tuple-element.60) | copy-start | bytes 12292
  207.3 30.3 %copy-start.9 = (f32[1,1024]{1,0:T(1,128)S(1)}, f32[1,1024]{1,0:T(1,128)}, u32[]{:S(2)}) copy-start(f32[1,1024]{1,0:T(1,128)} %get-tuple-element.61) | copy-start | bytes 12292
  207.3 30.3 %copy-start.11 = (f32[1,1024]{1,0:T(1,128)S(1)}, f32[1,1024]{1,0:T(1,128)}, u32[]{:S(2)}) copy-start(f32[1,1024]{1,0:T(1,128)} %get-tuple-element.62) | copy-start | bytes 12292
  207.3 30.3 %copy-start.16 = (f32[1,512]{1,0:T(1,128)S(1)}, f32[1,512]{1,0:T(1,128)}, u32[]{:S(2)}) copy-start(f32[1,512]{1,0:T(1,128)} %get-tuple-element.63) | copy-start | bytes 6148
  213.1 189.3 %collective-permute-start.5 = (bf16[1024,1024]{1,0:T(8,128)(2,1)S(1)}, bf16[1024,1024]{1,0:T(8,128)(2,1)}, u32[]{:S(2)}, u32[]{:S(2)}) collective-permute-start(bf16[1024,1024]{1,0:T(8,128)(2,1)S(1)} %copy-done), channel_id=1, source_target_pairs={{1,0},{0,1},{3,2},{2,3},{5,4},{4,5},{7,6},{6,7},{9,8},{8,9},{11,10... | collective-permute-start | bytes 6291464 | tf_op jit(solution)/shard_map/ppermute | solution.py:17
  238.9 166.5 %collective-permute-start.6 = (bf16[1024,1024]{1,0:T(8,128)(2,1)}, bf16[1024,1024]{1,0:T(8,128)(2,1)S(1)}, u32[]{:S(2)}, u32[]{:S(2)}) collective-permute-start(bf16[1024,1024]{1,0:T(8,128)(2,1)} %get-tuple-element.44.refs_0_), channel_id=1, source_target_pairs={{1,0},{0,1},{3,2},{2,3},{5,4},{4,5},{7,6},{6,7},{9,8},{8,9},{11,10... | collective-permute-start | bytes 6291464 | tf_op jit(solution)/shard_map/ppermute | solution.py:17
  242.7 164.2 %collective-permute-start.7 = (bf16[1024,1024]{1,0:T(8,128)(2,1)}, bf16[1024,1024]{1,0:T(8,128)(2,1)S(1)}, u32[]{:S(2)}, u32[]{:S(2)}) collective-permute-start(bf16[1024,1024]{1,0:T(8,128)(2,1)} %get-tuple-element.49.refs_0_), channel_id=1, source_target_pairs={{1,0},{0,1},{3,2},{2,3},{5,4},{4,5},{7,6},{6,7},{9,8},{8,9},{11,10... | collective-permute-start | bytes 6291464 | tf_op jit(solution)/shard_map/ppermute | solution.py:17
  243.2 158.1 %collective-permute-start.11 = (bf16[1024,512]{1,0:T(8,128)(2,1)}, bf16[1024,512]{1,0:T(8,128)(2,1)S(1)}, u32[]{:S(2)}, u32[]{:S(2)}) collective-permute-start(bf16[1024,512]{1,0:T(8,128)(2,1)} %get-tuple-element.51.refs_0_), channel_id=1, source_target_pairs={{1,0},{0,1},{3,2},{2,3},{5,4},{4,5},{7,6},{6,7},{9,8},{8,9},{11,10... | collective-permute-start | bytes 3145736 | tf_op jit(solution)/shard_map/ppermute | solution.py:17
  253.1 167.3 %collective-permute-start.12 = (bf16[1024,512]{1,0:T(8,128)(2,1)}, bf16[1024,512]{1,0:T(8,128)(2,1)S(1)}, u32[]{:S(2)}, u32[]{:S(2)}) collective-permute-start(bf16[1024,512]{1,0:T(8,128)(2,1)} %get-tuple-element.54.dep_ref), channel_id=1, source_target_pairs={{1,0},{0,1},{3,2},{2,3},{5,4},{4,5},{7,6},{6,7},{9,8},{8,9},{11,10... | collective-permute-start | bytes 3145736 | tf_op jit(solution)/shard_map/ppermute | solution.py:17

commit v2 on v1

--- a/solution.py
+++ b/solution.py
@@ -138,7 +138,7 @@
         at = me[None]
         experts, depth, width = w_gate.shape
         pairs = ((w_gate, avg_gate), (w_up, avg_up))
-        tile = math.gcd(depth, 256)
+        tile, tall = math.gcd(depth, 256), math.gcd(depth, 512)
         half = width // 2
 
         pieces = [(0, 0, 0, half), (0, 0, 1, half)]
@@ -165,17 +165,22 @@
         sent = send_piece(pieces[0], halves, 0, part)
 
         held = {}
-        last = sent
+
+        def sum_rest(which, first, count, dep):
+            part = sums(mix_share, *pairs[which], first, count, tall, dep)
+            got = halves_of(part, n)
+            for i in range(count):
+                held[which, first + i] = (got, i)
+            return part
+
+        last = sum_rest(1, 0, 1, sent)
+        last = send_piece(pieces[1], halves, 0, last)
         if experts > 1:
-            last = sums(mix_share, *pairs[0], 1, experts - 1, tile, last)
-            held[0] = halves_of(last, n)
-        last = sums(mix_share, *pairs[1], 0, experts, tile, last)
-        held[1] = halves_of(last, n)
-
-        last = send_piece(pieces[1], halves, 0, last)
-        for piece in pieces[2:]:
-            which, e = piece[:2]
-            last = send_piece(piece, held[which], e if which else e - 1, last)
+            last = sum_rest(0, 1, experts - 1, last)
+        for i, piece in enumerate(pieces[2:]):
+            last = send_piece(piece, *held[piece[:2]], last)
+            if i == 0 and experts > 1:
+                last = sum_rest(1, 1, experts - 1, last)
 
         moved = [shift(router, n, k) for k in range(1, n)]
         row_router = jnp.zeros((router.shape[0], n * depth), jnp.bfloat16)

time: 423 us -> 420 us (level)
    pallas_call x3 -> x4, Pallas kernels: 36 us -> 31.9 us  [sums(): pl.pallas_call(functools.partial(sum_kernel, first), grid=(count, depth /...]
    ppermute x14 -> x15, waiting for transfers between devices: 263 us -> 266 us  [shift(): return lax.ppermute(x, 'rows', [((j + k) % n, j) for j in range(n)])]
    ppermute x14 -> x15, starting transfers between devices: 17.1 us -> 16.2 us  [shift(): return lax.ppermute(x, 'rows', [((j + k) % n, j) for j in range(n)])]
  transfers between devices with their start and end apart: 14 -> 15, of which waited for: 4 -> 6; matrix products, arithmetic and copies ran while one was open for 6% -> 6% of each run, Pallas kernels for 12% -> 16%
where the time goes in v2:
time: 420 us; the launch traced here: 419 us
  waiting for transfers between devices  266 us (63%)
  Pallas kernels  87.3 us (21%)
  local copies, waits for them, and re-layouts  24.6 us (6%)
  blocking collectives  22.6 us (5%)
  starting transfers between devices  16.2 us (4%)
    ppermute x15, waiting for transfers between devices, shift(): return lax.ppermute(x, 'rows', [((j + k) % n, j) for j in range(n)])  266 us
    pallas_call x10, Pallas kernels, narrow(): pl.pallas_call(functools.partial(narrow_kernel, e), grid_spec=pltpu.Prefe...  52.7 us
    pallas_call x4, Pallas kernels, sums(): pl.pallas_call(functools.partial(sum_kernel, first), grid=(count, depth /...  31.9 us
    all_gather x1, blocking collectives, shards(): lax.all_gather(later(row_router, last), 'owner', axis=0, tiled=True)  22.6 us
    dynamic_update_slice x10, local copies, waits for them, and re-layouts, shards(): lax.dynamic_update_slice(outs[which], got[k - 1][None], (e, lax.rem(me +...  21.9 us
    ppermute x15, starting transfers between devices, shift(): return lax.ppermute(x, 'rows', [((j + k) % n, j) for j in range(n)])  16.2 us
  transfers between devices with their start and end apart: 15, of which 6 were waited for; matrix products, arithmetic and copies ran while one was open for 6% of the time, Pallas kernels for 16%

profile of v2, /device:TPU:0, one launch (start us, length us, event | category | flops | bytes accessed | tf_op | source)
XLA Modules:
  0.0 419.3 jit_solution(15644039128765622428)
XLA Ops:
  0.6 5.1 %shard_map.110.a_ref.refs_0_.dep_ref = f32[1,1,1024]{2,1,0:T(1,128)} custom-call(f32[4]{0:T(128)} %share_ref.27, f32[4,1024,1024]{2,1,0:T(8,128)} %w_ref.25, f32[4,1024,1024]{2,1,0:T(8,128)} %avg_ref.25, f32[4]{0:T(128)} %share_ref.27), custom_call_target="tpu_custom_call" | custom-call | flops 5242880 | bytes 8388608 | tf_op jit(solution)/shard_map/pallas_call | solution.py:50
  5.8 3.0 collective-permute-start
  8.7 1.8 collective-permute-done.b_ref
  10.5 0.6 copy-done.10
  11.1 4.2 %shard_map.111 = (bf16[1024,512]{1,0:T(8,128)(2,1)}, f32[1,512]{1,0:T(1,128)}, bf16[4,2048,1024]{2,1,0:T(8,128)(2,1)}) custom-call(s32[1]{0:T(128)} %bitcast.me_ref, f32[4]{0:T(128)} %share_ref.27, f32[4,1024,1024]{2,1,0:T(8,128)} %w_ref.25, f32[4,1024,1024]{2,1,0:T(8,128)} %avg_ref.25, f32[1,1,1024]{2,1,0:T(1,128)} %shard_map.110.a_ref.refs_0_.dep_ref, ...), custom_call_target="tpu_custom_call" | custom-call | flops 4194304 | bytes 6291456 | tf_op jit(solution)/shard_map/pallas_call | solution.py:85
  15.4 4.7 %shard_map.112.refs_0_.a_ref = f32[1,1,1024]{2,1,0:T(1,128)} custom-call(f32[4]{0:T(128)} %share_ref.27, f32[4,1024,1024]{2,1,0:T(8,128)} %w_ref.27, f32[4,1024,1024]{2,1,0:T(8,128)} %avg_ref.27, bf16[1024,512]{1,0:T(8,128)(2,1)} %get-tuple-element.35.dep_ref), custom_call_target="tpu_custom_call" | custom-call | flops 5242880 | bytes 8388608 | tf_op jit(solution)/shard_map/pallas_call | solution.py:50
  20.1 2.0 collective-permute-start.2
  22.1 4.2 %shard_map.113 = (bf16[1024,512]{1,0:T(8,128)(2,1)}, f32[1,512]{1,0:T(1,128)}, bf16[4,2048,1024]{2,1,0:T(8,128)(2,1)}) custom-call(s32[1]{0:T(128)} %bitcast.me_ref, f32[4]{0:T(128)} %share_ref.27, f32[4,1024,1024]{2,1,0:T(8,128)} %w_ref.25, f32[4,1024,1024]{2,1,0:T(8,128)} %avg_ref.25, ...), custom_call_target="tpu_custom_call", output_to_operand_aliasing={{2}: (7, {})} | custom-call | flops 4194304 | bytes 6291456 | tf_op jit(solution)/shard_map/pallas_call | solution.py:85
  26.4 11.1 %shard_map.114.refs_0_.a_ref = f32[3,1,1024]{2,1,0:T(1,128)} custom-call(f32[4]{0:T(128)} %share_ref.27, f32[4,1024,1024]{2,1,0:T(8,128)} %w_ref.25, f32[4,1024,1024]{2,1,0:T(8,128)} %avg_ref.25, bf16[1024,512]{1,0:T(8,128)(2,1)} %get-tuple-element.37.dep_ref), custom_call_target="tpu_custom_call" | custom-call | flops 15728640 | bytes 25165824 | tf_op jit(solution)/shard_map/pallas_call | solution.py:50
  37.4 0.0 collective-permute-done.2.b_ref
  37.4 0.0 copy-start.11
  37.4 0.6 copy-done.11
  38.0 5.9 %shard_map.115 = (bf16[1024,1024]{1,0:T(8,128)(2,1)}, f32[1,1024]{1,0:T(1,128)}, bf16[4,2048,1024]{2,1,0:T(8,128)(2,1)}) custom-call(s32[1]{0:T(128)} %bitcast.me_ref, f32[4]{0:T(128)} %share_ref.27, f32[4,1024,1024]{2,1,0:T(8,128)} %w_ref.27, f32[4,1024,1024]{2,1,0:T(8,128)} %avg_ref.27, f32[1,1,1024]{2,1,0:T(1,128)} %shard_map.112.refs_0_.a_ref, ...), custom_call_target="tpu_custom_call" | custom-call | flops 8388608 | bytes 12582912 | tf_op jit(solution)/shard_map/pallas_call | solution.py:85
  43.9 0.0 collective-permute-start.9
  43.9 2.0 collective-permute-start.4
  46.0 0.1 collective-permute-start.1
  46.0 11.0 %shard_map.116.refs_0_.a_ref = f32[3,1,1024]{2,1,0:T(1,128)} custom-call(f32[4]{0:T(128)} %share_ref.27, f32[4,1024,1024]{2,1,0:T(8,128)} %w_ref.27, f32[4,1024,1024]{2,1,0:T(8,128)} %avg_ref.27, bf16[1024,1024]{1,0:T(8,128)(2,1)} %get-tuple-element.38.dep_ref), custom_call_target="tpu_custom_call" | custom-call | flops 15728640 | bytes 25165824 | tf_op jit(solution)/shard_map/pallas_call | solution.py:50
  57.1 55.7 %collective-permute-done.1.b_ref = f32[3,1,1024]{2,1,0:T(1,128)S(1)} collective-permute-done((f32[3,1,1024]{2,1,0:T(1,128)S(1)}, f32[3,1,1024]{2,1,0:T(1,128)S(1)}, u32[]{:S(2)}, u32[]{:S(2)}) %collective-permute-start.1) | collective-permute-done | bytes 12320 | tf_op jit(solution)/shard_map/ppermute | solution.py:17
  112.8 0.6 copy-done.7
  113.4 6.0 %shard_map.117 = (bf16[1024,1024]{1,0:T(8,128)(2,1)}, f32[1,1024]{1,0:T(1,128)}, bf16[4,2048,1024]{2,1,0:T(8,128)(2,1)}) custom-call(s32[1]{0:T(128)} %bitcast.me_ref, f32[4]{0:T(128)} %share_ref.27, f32[4,1024,1024]{2,1,0:T(8,128)} %w_ref.25, f32[4,1024,1024]{2,1,0:T(8,128)} %avg_ref.25, ...), custom_call_target="tpu_custom_call", output_to_operand_aliasing={{2}: (7, {})} | custom-call | flops 8388608 | bytes 12582912 | tf_op jit(solution)/shard_map/pallas_call | solution.py:85
  119.4 0.3 collective-permute-start.6
  119.7 1.7 collective-permute-start.5
  121.4 0.3 collective-permute-start.3
  121.7 1.3 shard_map.124
  123.1 64.5 %collective-permute-done.3.b_ref = f32[3,1,1024]{2,1,0:T(1,128)S(1)} collective-permute-done((f32[3,1,1024]{2,1,0:T(1,128)S(1)}, f32[3,1,1024]{2,1,0:T(1,128)S(1)}, u32[]{:S(2)}, u32[]{:S(2)}) %collective-permute-start.3) | collective-permute-done | bytes 12320 | tf_op jit(solution)/shard_map/ppermute | solution.py:17
  187.5 0.6 collective-permute-start.14
  188.1 0.0 copy-done.6
  188.1 5.9 %shard_map.118 = (bf16[1024,1024]{1,0:T(8,128)(2,1)}, f32[1,1024]{1,0:T(1,128)}, bf16[4,2048,1024]{2,1,0:T(8,128)(2,1)}) custom-call(s32[1]{0:T(128)} %bitcast.me_ref, f32[4]{0:T(128)} %share_ref.27, f32[4,1024,1024]{2,1,0:T(8,128)} %w_ref.27, f32[4,1024,1024]{2,1,0:T(8,128)} %avg_ref.27, ...), custom_call_target="tpu_custom_call", output_to_operand_aliasing={{2}: (7, {})} | custom-call | flops 8388608 | bytes 12582912 | tf_op jit(solution)/shard_map/pallas_call | solution.py:85
  194.0 0.0 collective-permute-done.14
  194.0 1.5 collective-permute-start.10
  195.5 5.9 %shard_map.119 = (bf16[1024,1024]{1,0:T(8,128)(2,1)}, f32[1,1024]{1,0:T(1,128)}, bf16[4,2048,1024]{2,1,0:T(8,128)(2,1)}) custom-call(s32[1]{0:T(128)} %bitcast.me_ref, f32[4]{0:T(128)} %share_ref.27, f32[4,1024,1024]{2,1,0:T(8,128)} %w_ref.25, f32[4,1024,1024]{2,1,0:T(8,128)} %avg_ref.25, ...), custom_call_target="tpu_custom_call", output_to_operand_aliasing={{2}: (7, {})} | custom-call | flops 8388608 | bytes 12582912 | tf_op jit(solution)/shard_map/pallas_call | solution.py:85
  201.4 5.9 %shard_map.120 = (bf16[1024,1024]{1,0:T(8,128)(2,1)}, f32[1,1024]{1,0:T(1,128)}, bf16[4,2048,1024]{2,1,0:T(8,128)(2,1)}) custom-call(s32[1]{0:T(128)} %bitcast.me_ref, f32[4]{0:T(128)} %share_ref.27, f32[4,1024,1024]{2,1,0:T(8,128)} %w_ref.27, f32[4,1024,1024]{2,1,0:T(8,128)} %avg_ref.27, ...), custom_call_target="tpu_custom_call", output_to_operand_aliasing={{2}: (7, {})} | custom-call | flops 8388608 | bytes 12582912 | tf_op jit(solution)/shard_map/pallas_call | solution.py:85
  207.3 0.0 collective-permute-done.4
  207.4 0.6 collective-permute-start.11
  208.1 0.0 copy-start.8
  208.1 5.9 %shard_map.121 = (bf16[1024,1024]{1,0:T(8,128)(2,1)}, f32[1,1024]{1,0:T(1,128)}, bf16[4,2048,1024]{2,1,0:T(8,128)(2,1)}) custom-call(s32[1]{0:T(128)} %bitcast.me_ref, f32[4]{0:T(128)} %share_ref.27, f32[4,1024,1024]{2,1,0:T(8,128)} %w_ref.25, f32[4,1024,1024]{2,1,0:T(8,128)} %avg_ref.25, ...), custom_call_target="tpu_custom_call", output_to_operand_aliasing={{2}: (7, {})} | custom-call | flops 8388608 | bytes 12582912 | tf_op jit(solution)/shard_map/pallas_call | solution.py:85
  214.0 4.3 %shard_map.122 = (bf16[1024,512]{1,0:T(8,128)(2,1)}, f32[1,512]{1,0:T(1,128)}, bf16[4,2048,1024]{2,1,0:T(8,128)(2,1)}) custom-call(s32[1]{0:T(128)} %bitcast.me_ref, f32[4]{0:T(128)} %share_ref.27, f32[4,1024,1024]{2,1,0:T(8,128)} %w_ref.27, f32[4,1024,1024]{2,1,0:T(8,128)} %avg_ref.27, ...), custom_call_target="tpu_custom_call", output_to_operand_aliasing={{2}: (7, {})} | custom-call | flops 4194304 | bytes 6291456 | tf_op jit(solution)/shard_map/pallas_call | solution.py:85
  218.4 4.4 %shard_map.123 = (bf16[1024,512]{1,0:T(8,128)(2,1)}, f32[1,512]{1,0:T(1,128)}, bf16[4,2048,1024]{2,1,0:T(8,128)(2,1)}) custom-call(s32[1]{0:T(128)} %bitcast.me_ref, f32[4]{0:T(128)} %share_ref.27, f32[4,1024,1024]{2,1,0:T(8,128)} %w_ref.27, f32[4,1024,1024]{2,1,0:T(8,128)} %avg_ref.27, ...), custom_call_target="tpu_custom_call", output_to_operand_aliasing={{2}: (7, {})} | custom-call | flops 4194304 | bytes 6291456 | tf_op jit(solution)/shard_map/pallas_call | solution.py:85
  222.8 1.3 shard_map.125
  224.1 22.6 %all-gather = bf16[16,4,2048]{2,1,0:T(4,128)(2,1)S(1)} all-gather(bf16[1,4,2048]{2,1,0:T(4,128)(2,1)} %bitcast.26), channel_id=1, replica_groups=mesh['owner'=16,'rows'=2] {'owner'}, dimensions={0}, use_global_device_ids=true | all-gather | bytes 278528 | tf_op jit(solution)/shard_map/all_gather | solution.py:192
  246.7 0.8 reshape.11
  247.5 0.6 pad_maximum_fusion
  248.1 1.3 maximum_maximum_fusion
  249.4 0.0 collective-permute-done.5
  249.4 1.4 collective-permute-start.7
  250.9 2.3 bitcast_dynamic-update-slice_fusion.9
  253.2 0.6 collective-permute-start.8
  253.7 2.3 bitcast_dynamic-update-slice_fusion.8
  256.0 0.0 collective-permute-done.6
  256.0 1.4 collective-permute-start.12
  257.4 3.1 bitcast_dynamic-update-slice_fusion.2
  260.5 3.1 bitcast_dynamic-update-slice_fusion.5
  263.6 0.0 collective-permute-done.10
  263.6 0.6 collective-permute-start.13
  264.2 3.1 bitcast_dynamic-update-slice_fusion.1
  267.3 20.6 %collective-permute-done.11 = bf16[1024,1024]{1,0:T(8,128)(2,1)} collective-permute-done((bf16[1024,1024]{1,0:T(8,128)(2,1)}, bf16[1024,1024]{1,0:T(8,128)(2,1)}, u32[]{:S(2)}, u32[]{:S(2)}) %collective-permute-start.11) | collective-permute-done | bytes 2097184 | tf_op jit(solution)/shard_map/ppermute | solution.py:17
  287.8 3.1 bitcast_dynamic-update-slice_fusion
  290.9 109.2 %collective-permute-done.12 = bf16[1024,512]{1,0:T(8,128)(2,1)S(1)} collective-permute-done((bf16[1024,512]{1,0:T(8,128)(2,1)}, bf16[1024,512]{1,0:T(8,128)(2,1)S(1)}, u32[]{:S(2)}, u32[]{:S(2)}) %collective-permute-start.12) | collective-permute-done | bytes 1048608 | tf_op jit(solution)/shard_map/ppermute | solution.py:17
  400.1 1.0 bitcast_dynamic-update-slice_fusion.7
  401.1 0.0 collective-permute-done.7
  401.1 1.5 bitcast_dynamic-update-slice_fusion.4
  402.6 1.5 bitcast_dynamic-update-slice_fusion.3
  404.1 14.2 %collective-permute-done.13 = bf16[1024,512]{1,0:T(8,128)(2,1)S(1)} collective-permute-done((bf16[1024,512]{1,0:T(8,128)(2,1)}, bf16[1024,512]{1,0:T(8,128)(2,1)S(1)}, u32[]{:S(2)}, u32[]{:S(2)}) %collective-permute-start.13) | collective-permute-done | bytes 1048608 | tf_op jit(solution)/shard_map/ppermute | solution.py:17
  418.3 1.0 bitcast_dynamic-update-slice_fusion.6
  (41 shorter events, 0.1 us)
Async XLA Ops:
  5.8 4.8 %collective-permute-start = (f32[1,1,1024]{2,1,0:T(1,128)}, f32[1,1,1024]{2,1,0:T(1,128)S(1)}, u32[]{:S(2)}, u32[]{:S(2)}) collective-permute-start(f32[1,1,1024]{2,1,0:T(1,128)} %shard_map.110.a_ref.refs_0_.dep_ref), channel_id=1, source_target_pairs={{1,0},{0,1},{3,2},{2,3},{5,4},{4,5},{7,6},{6,7},{9,8},{8,9},{11,10... | collective-permute-start | bytes 12296 | tf_op jit(solution)/shard_map/ppermute | solution.py:17
  10.5 0.6 copy-start.10
  20.1 17.3 %collective-permute-start.2 = (f32[1,1,1024]{2,1,0:T(1,128)}, f32[1,1,1024]{2,1,0:T(1,128)S(1)}, u32[]{:S(2)}, u32[]{:S(2)}) collective-permute-start(f32[1,1,1024]{2,1,0:T(1,128)} %shard_map.112.refs_0_.a_ref), channel_id=1, source_target_pairs={{1,0},{0,1},{3,2},{2,3},{5,4},{4,5},{7,6},{6,7},{9,8},{8,9},{11,10... | collective-permute-start | bytes 12296 | tf_op jit(solution)/shard_map/ppermute | solution.py:17
  37.4 6.5 %copy-start.2 = (bf16[1024,512]{1,0:T(8,128)(2,1)S(1)}, bf16[1024,512]{1,0:T(8,128)(2,1)}, u32[]{:S(2)}) copy-start(bf16[1024,512]{1,0:T(8,128)(2,1)} %get-tuple-element.35.dep_ref) | copy-start | bytes 3145732
  37.4 8.5 %copy-start.5 = (f32[3,1,1024]{2,1,0:T(1,128)S(1)}, f32[3,1,1024]{2,1,0:T(1,128)}, u32[]{:S(2)}) copy-start(f32[3,1,1024]{2,1,0:T(1,128)} %shard_map.114.refs_0_.a_ref) | copy-start | bytes 36868
  37.4 0.6 copy-start.11
  43.9 209.2 %collective-permute-start.9 = (bf16[1024,1024]{1,0:T(8,128)(2,1)}, bf16[1024,1024]{1,0:T(8,128)(2,1)}, u32[]{:S(2)}, u32[]{:S(2)}) collective-permute-start(bf16[1024,1024]{1,0:T(8,128)(2,1)} %get-tuple-element.38.dep_ref), channel_id=1, source_target_pairs={{1,0},{0,1},{3,2},{2,3},{5,4},{4,5},{7,6},{6,7},{9,8},{8,9},{11,10... | collective-permute-start | bytes 6291464 | tf_op jit(solution)/shard_map/ppermute | solution.py:17
  43.9 163.4 %collective-permute-start.4 = (bf16[1024,512]{1,0:T(8,128)(2,1)S(1)}, bf16[1024,512]{1,0:T(8,128)(2,1)S(1)}, u32[]{:S(2)}, u32[]{:S(2)}) collective-permute-start(bf16[1024,512]{1,0:T(8,128)(2,1)S(1)} %copy-done.2), channel_id=1, source_target_pairs={{1,0},{0,1},{3,2},{2,3},{5,4},{4,5},{7,6},{6,7},{9,8},{8,9},{11,10... | collective-permute-start | bytes 3145736 | tf_op jit(solution)/shard_map/ppermute | solution.py:17
  46.0 66.9 %collective-permute-start.1 = (f32[3,1,1024]{2,1,0:T(1,128)S(1)}, f32[3,1,1024]{2,1,0:T(1,128)S(1)}, u32[]{:S(2)}, u32[]{:S(2)}) collective-permute-start(f32[3,1,1024]{2,1,0:T(1,128)S(1)} %copy-done.5), channel_id=1, source_target_pairs={{1,0},{0,1},{3,2},{2,3},{5,4},{4,5},{7,6},{6,7},{9,8},{8,9},{11,10... | collective-permute-start | bytes 36872 | tf_op jit(solution)/shard_map/ppermute | solution.py:17
  112.8 0.6 copy-start.7
  113.4 6.3 %copy-start.1 = (bf16[1024,512]{1,0:T(8,128)(2,1)S(1)}, bf16[1024,512]{1,0:T(8,128)(2,1)}, u32[]{:S(2)}) copy-start(bf16[1024,512]{1,0:T(8,128)(2,1)} %get-tuple-element.37.dep_ref) | copy-start | bytes 3145732
  113.4 8.0 %copy-start.4 = (f32[3,1,1024]{2,1,0:T(1,128)S(1)}, f32[3,1,1024]{2,1,0:T(1,128)}, u32[]{:S(2)}) copy-start(f32[3,1,1024]{2,1,0:T(1,128)} %shard_map.116.refs_0_.a_ref) | copy-start | bytes 36868
  119.4 136.6 %collective-permute-start.6 = (bf16[1024,1024]{1,0:T(8,128)(2,1)}, bf16[1024,1024]{1,0:T(8,128)(2,1)}, u32[]{:S(2)}, u32[]{:S(2)}) collective-permute-start(bf16[1024,1024]{1,0:T(8,128)(2,1)} %get-tuple-element.40.refs_0_), channel_id=1, source_target_pairs={{1,0},{0,1},{3,2},{2,3},{5,4},{4,5},{7,6},{6,7},{9,8},{8,9},{11,10... | collective-permute-start | bytes 6291464 | tf_op jit(solution)/shard_map/ppermute | solution.py:17
  119.7 129.7 %collective-permute-start.5 = (bf16[1024,512]{1,0:T(8,128)(2,1)S(1)}, bf16[1024,512]{1,0:T(8,128)(2,1)}, u32[]{:S(2)}, u32[]{:S(2)}) collective-permute-start(bf16[1024,512]{1,0:T(8,128)(2,1)S(1)} %copy-done.1), channel_id=1, source_target_pairs={{1,0},{0,1},{3,2},{2,3},{5,4},{4,5},{7,6},{6,7},{9,8},{8,9},{11,10... | collective-permute-start | bytes 3145736 | tf_op jit(solution)/shard_map/ppermute | solution.py:17
  121.4 66.1 %collective-permute-start.3 = (f32[3,1,1024]{2,1,0:T(1,128)S(1)}, f32[3,1,1024]{2,1,0:T(1,128)S(1)}, u32[]{:S(2)}, u32[]{:S(2)}) collective-permute-start(f32[3,1,1024]{2,1,0:T(1,128)S(1)} %copy-done.4), channel_id=1, source_target_pairs={{1,0},{0,1},{3,2},{2,3},{5,4},{4,5},{7,6},{6,7},{9,8},{8,9},{11,10... | collective-permute-start | bytes 36872 | tf_op jit(solution)/shard_map/ppermute | solution.py:17
  187.5 0.6 copy-start.6
  187.5 6.5 %collective-permute-start.14 = (bf16[4,1024]{1,0:T(4,128)(2,1)}, bf16[4,1024]{1,0:T(4,128)(2,1)S(1)}, u32[]{:S(2)}, u32[]{:S(2)}) collective-permute-start(bf16[4,1024]{1,0:T(4,128)(2,1)} %shard_map.124), channel_id=1, source_target_pairs={{1,0},{0,1},{3,2},{2,3},{5,4},{4,5},{7,6},{6,7},{9,8},{8,9},{11,10... | collective-permute-start | bytes 24584 | tf_op jit(solution)/shard_map/ppermute | solution.py:17
  194.0 69.6 %collective-permute-start.10 = (bf16[1024,1024]{1,0:T(8,128)(2,1)}, bf16[1024,1024]{1,0:T(8,128)(2,1)}, u32[]{:S(2)}, u32[]{:S(2)}) collective-permute-start(bf16[1024,1024]{1,0:T(8,128)(2,1)} %get-tuple-element.42.refs_0_), channel_id=1, source_target_pairs={{1,0},{0,1},{3,2},{2,3},{5,4},{4,5},{7,6},{6,7},{9,8},{8,9},{11,10... | collective-permute-start | bytes 6291464 | tf_op jit(solution)/shard_map/ppermute | solution.py:17
  201.4 6.6 %copy-start.9 = (bf16[4,1024]{1,0:T(4,128)(2,1)S(1)}, bf16[4,1024]{1,0:T(4,128)(2,1)}, u32[]{:S(2)}) copy-start(bf16[4,1024]{1,0:T(4,128)(2,1)} %shard_map.124) | copy-start | bytes 24580
  207.3 6.7 %copy-start.3 = (bf16[1024,512]{1,0:T(8,128)(2,1)}, bf16[1024,512]{1,0:T(8,128)(2,1)S(1)}, u32[]{:S(2)}) copy-start(bf16[1024,512]{1,0:T(8,128)(2,1)S(1)} %collective-permute-done.4) | copy-start | bytes 3145732
  207.4 80.5 %collective-permute-start.11 = (bf16[1024,1024]{1,0:T(8,128)(2,1)}, bf16[1024,1024]{1,0:T(8,128)(2,1)}, u32[]{:S(2)}, u32[]{:S(2)}) collective-permute-start(bf16[1024,1024]{1,0:T(8,128)(2,1)} %get-tuple-element.46.refs_0_), channel_id=1, source_target_pairs={{1,0},{0,1},{3,2},{2,3},{5,4},{4,5},{7,6},{6,7},{9,8},{8,9},{11,10... | collective-permute-start | bytes 6291464 | tf_op jit(solution)/shard_map/ppermute | solution.py:17
  208.1 5.9 %copy-start.8 = (bf16[4,2048]{1,0:T(4,128)(2,1)}, bf16[4,2048]{1,0:T(4,128)(2,1)S(1)}, u32[]{:S(2)}) copy-start(bf16[4,2048]{1,0:T(4,128)(2,1)S(1)} %constant_dynamic-update-slice_fusion.x_ref) | copy-start | bytes 49156
  218.3 29.2 %copy-start.13 = (f32[1,1024]{1,0:T(1,128)S(1)}, f32[1,1024]{1,0:T(1,128)}, u32[]{:S(2)}) copy-start(f32[1,1024]{1,0:T(1,128)} %get-tuple-element.57) | copy-start | bytes 12292
  218.3 29.2 %copy-start.16 = (f32[1,1024]{1,0:T(1,128)S(1)}, f32[1,1024]{1,0:T(1,128)}, u32[]{:S(2)}) copy-start(f32[1,1024]{1,0:T(1,128)} %get-tuple-element.58) | copy-start | bytes 12292
  218.3 29.2 %copy-start.17 = (f32[1,1024]{1,0:T(1,128)S(1)}, f32[1,1024]{1,0:T(1,128)}, u32[]{:S(2)}) copy-start(f32[1,1024]{1,0:T(1,128)} %get-tuple-element.59) | copy-start | bytes 12292
  218.3 29.2 %copy-start.18 = (f32[1,512]{1,0:T(1,128)S(1)}, f32[1,512]{1,0:T(1,128)}, u32[]{:S(2)}) copy-start(f32[1,512]{1,0:T(1,128)} %get-tuple-element.55) | copy-start | bytes 6148
  218.3 29.2 %copy-start.19 = (f32[1,512]{1,0:T(1,128)S(1)}, f32[1,512]{1,0:T(1,128)}, u32[]{:S(2)}) copy-start(f32[1,512]{1,0:T(1,128)} %get-tuple-element.56) | copy-start | bytes 6148
  218.3 29.8 %copy-start.12 = (f32[1,1024]{1,0:T(1,128)S(1)}, f32[1,1024]{1,0:T(1,128)}, u32[]{:S(2)}) copy-start(f32[1,1024]{1,0:T(1,128)} %get-tuple-element.60) | copy-start | bytes 12292
  218.3 29.8 %copy-start.14 = (f32[1,1024]{1,0:T(1,128)S(1)}, f32[1,1024]{1,0:T(1,128)}, u32[]{:S(2)}) copy-start(f32[1,1024]{1,0:T(1,128)} %get-tuple-element.61) | copy-start | bytes 12292
  218.3 29.8 %copy-start.15 = (f32[1,1024]{1,0:T(1,128)S(1)}, f32[1,1024]{1,0:T(1,128)}, u32[]{:S(2)}) copy-start(f32[1,1024]{1,0:T(1,128)} %get-tuple-element.62) | copy-start | bytes 12292
  218.4 29.8 %copy-start.20 = (f32[1,512]{1,0:T(1,128)S(1)}, f32[1,512]{1,0:T(1,128)}, u32[]{:S(2)}) copy-start(f32[1,512]{1,0:T(1,128)} %get-tuple-element.63) | copy-start | bytes 6148
  218.4 31.1 %copy-start = (bf16[1024,1024]{1,0:T(8,128)(2,1)S(1)}, bf16[1024,1024]{1,0:T(8,128)(2,1)}, u32[]{:S(2)}) copy-start(bf16[1024,1024]{1,0:T(8,128)(2,1)} %get-tuple-element.44.refs_0_) | copy-start | bytes 6291460
  249.4 151.7 %collective-permute-start.7 = (bf16[1024,1024]{1,0:T(8,128)(2,1)S(1)}, bf16[1024,1024]{1,0:T(8,128)(2,1)S(1)}, u32[]{:S(2)}, u32[]{:S(2)}) collective-permute-start(bf16[1024,1024]{1,0:T(8,128)(2,1)S(1)} %copy-done), channel_id=1, source_target_pairs={{1,0},{0,1},{3,2},{2,3},{5,4},{4,5},{7,6},{6,7},{9,8},{8,9},{11,10... | collective-permute-start | bytes 6291464 | tf_op jit(solution)/shard_map/ppermute | solution.py:17
  253.2 149.5 %collective-permute-start.8 = (bf16[1024,1024]{1,0:T(8,128)(2,1)}, bf16[1024,1024]{1,0:T(8,128)(2,1)S(1)}, u32[]{:S(2)}, u32[]{:S(2)}) collective-permute-start(bf16[1024,1024]{1,0:T(8,128)(2,1)} %get-tuple-element.49.refs_0_), channel_id=1, source_target_pairs={{1,0},{0,1},{3,2},{2,3},{5,4},{4,5},{7,6},{6,7},{9,8},{8,9},{11,10... | collective-permute-start | bytes 6291464 | tf_op jit(solution)/shard_map/ppermute | solution.py:17
  256.0 144.1 %collective-permute-start.12 = (bf16[1024,512]{1,0:T(8,128)(2,1)}, bf16[1024,512]{1,0:T(8,128)(2,1)S(1)}, u32[]{:S(2)}, u32[]{:S(2)}) collective-permute-start(bf16[1024,512]{1,0:T(8,128)(2,1)} %get-tuple-element.51.refs_0_), channel_id=1, source_target_pairs={{1,0},{0,1},{3,2},{2,3},{5,4},{4,5},{7,6},{6,7},{9,8},{8,9},{11,10... | collective-permute-start | bytes 3145736 | tf_op jit(solution)/shard_map/ppermute | solution.py:17
  263.6 154.7 %collective-permute-start.13 = (bf16[1024,512]{1,0:T(8,128)(2,1)}, bf16[1024,512]{1,0:T(8,128)(2,1)S(1)}, u32[]{:S(2)}, u32[]{:S(2)}) collective-permute-start(bf16[1024,512]{1,0:T(8,128)(2,1)} %get-tuple-element.54.dep_ref), channel_id=1, source_target_pairs={{1,0},{0,1},{3,2},{2,3},{5,4},{4,5},{7,6},{6,7},{9,8},{8,9},{11,10... | collective-permute-start | bytes 3145736 | tf_op jit(solution)/shard_map/ppermute | solution.py:17
